TPU v7x, 768 devices: a whole 4x8x12 slice. The times are simulated.
768 devices in a mesh: gx: 96 (over y, z_hi, x), gy: 8 (over z_lo, core).
Axes of the slice: x: 4, y: 8, z: 12 (z_hi: 3, z_lo: 4; z = z_hi * 4 + z_lo), core: 2. Of those that a mesh axis runs over, the one named last changes fastest.
Arguments:
- u_now_c: float32 [3, 192, 32, 128], P(None, 'gx', 'gy'), may hold values from -6 to 6
- u_prev_c: float32 [3, 192, 32, 128], P(None, 'gx', 'gy'), may hold values from -6 to 6
- memory_c: float32 [3, 3, 192, 32, 128], P(None, None, 'gx', 'gy'), may hold values from -3 to 3
- mu_c: float32 [192, 32, 128], P('gx', 'gy'), may hold values from 0.5 to 1.5
- lam_c: float32 [192, 32, 128], P('gx', 'gy'), may hold values from 0.5 to 1.5
- rho_c: float32 [192, 32, 128], P('gx', 'gy'), may hold values from 1 to 2
- q_c: float32 [3, 192, 32, 128], P(None, 'gx', 'gy'), may hold values from 0.05 to 0.4
- omega_c: float32 [3, 192, 32, 128], P(None, 'gx', 'gy'), may hold values from 0.1 to 8
- u_now_f: float32 [3, 384, 64, 128], P(None, 'gx', 'gy'), may hold values from -6 to 6
- u_prev_f: float32 [3, 384, 64, 128], P(None, 'gx', 'gy'), may hold values from -6 to 6
- memory_f: float32 [3, 3, 384, 64, 128], P(None, None, 'gx', 'gy'), may hold values from -3 to 3
- mu_f: float32 [384, 64, 128], P('gx', 'gy'), may hold values from 0.5 to 1.5
- lam_f: float32 [384, 64, 128], P('gx', 'gy'), may hold values from 0.5 to 1.5
- rho_f: float32 [384, 64, 128], P('gx', 'gy'), may hold values from 1 to 2
- q_f: float32 [3, 384, 64, 128], P(None, 'gx', 'gy'), may hold values from 0.05 to 0.4
- omega_f: float32 [3, 384, 64, 128], P(None, 'gx', 'gy'), may hold values from 0.1 to 8
- stretch_f: float32 [384, 64], P('gx', 'gy'), may hold values from 0.35 to 0.7
Outputs:
- u_out_c: float32 [3, 192, 32, 128], P(None, 'gx', 'gy')
- u_out_f: float32 [3, 384, 64, 128], P(None, 'gx', 'gy')
- memory_out_c: float32 [3, 3, 192, 32, 128], P(None, None, 'gx', 'gy')
- memory_out_f: float32 [3, 3, 384, 64, 128], P(None, None, 'gx', 'gy')
All inputs are finite; a program needn't handle non-finite values.
Results may differ from a plain program's by a relative error of at most 0.0001.
Values sent between devices are 32-bit elements; how exact they have to be, the bound alone decides.
No kernel may reach another device: no remote copies, remote signals or barrier semaphores. Data moves between devices by JAX's collectives and lax.ppermute only.
A program may use at most 32 MiB of HBM per device.

v0:
```python
import jax
import jax.numpy as jnp
from jax import lax
from jax.experimental import pallas as pl
from jax.experimental.pallas import tpu as pltpu
from jax.sharding import PartitionSpec as P

DT = 0.1
F32 = jnp.float32
LANES = 128


def layout(pieces):
    table, at = {}, 0
    for key, rows in pieces:
        table[key] = (at, rows)
        at += rows
    return table, -(-at // 8) * 8


X_AT, X_ROWS = layout(
    [(("f", c, r), 8) for r in (1, 2) for c in range(3)]
    + [(("f", f, 1), 8) for f in range(3, 8)]
    + [("bits", 8)]
    + [(("c", c, x), 4) for c in range(3) for x in range(2)]
    + [(("c", f, None), 4) for f in range(3, 8)]
)
Y_F = (
    [(("f", c, x), 4) for c in range(3) for x in range(-2, 6)]
    + [(("bits", side), 4) for side in range(2)]
    + [(("f", f, x), 2) for f in range(3, 8) for x in range(-1, 5)]
    + [(("f", 8, x), 2) for x in range(4)]
)
Y_C = [(("c", c, x), 2) for c in range(3) for x in range(-2, 4)] + [
    (("c", f, x), 2) for f in range(3, 8) for x in range(-1, 3)
]
Y_AT, Y_ROWS = layout(Y_F + Y_C)


def lane_roll(tile, by):
    return pltpu.roll(tile, by % LANES, axis=1)


def row_roll(tile, by):
    return pltpu.roll(tile, by % tile.shape[0], axis=0)


def relax(u, mem, q, om):
    nxt = [[mem[l][c] + DT * om[l] * (u[c] - mem[l][c]) for c in range(3)] for l in range(3)]
    old = [sum(q[l] * mem[l][c] for l in range(3)) for c in range(3)]
    new = [sum(q[l] * nxt[l][c] for l in range(3)) for c in range(3)]
    return old, nxt, new


def pre_kernel(uc, pc, mc, muc, lamc, rhoc, qc, omc, uf, pf, mf, muf, lamf, rhof, qf, omf, st, inner, outer, own_f, own_c):
    even = lax.rem(lax.axis_index("gx"), 2) == 0
    eye = lax.broadcasted_iota(jnp.int32, (8, 8), 0) == lax.broadcasted_iota(jnp.int32, (8, 8), 1)
    lane = lax.broadcasted_iota(jnp.int32, (8, LANES), 1)

    def level(u_r, p_r, m_r, mu_r, lam_r, rho_r, q_r, om_r, own, wide):
        for x in range(wide):
            u = [u_r[c, x] for c in range(3)]
            mem = [[m_r[l, c, x] for c in range(3)] for l in range(3)]
            old, _, new = relax(u, mem, [q_r[l, x] for l in range(3)], [om_r[l, x] for l in range(3)])
            scale = (DT * DT) / rho_r[x]
            mu = mu_r[x]
            for c in range(3):
                own[c * wide + x] = u[c] - old[c]
                own[(3 + c) * wide + x] = 2.0 * u[c] - p_r[c, x] - new[c]
            own[6 * wide + x] = scale * mu
            own[7 * wide + x] = scale * (lam_r[x] + mu)

    level(uf, pf, mf, muf, lamf, rhof, qf, omf, own_f, 4)
    level(uc, pc, mc, muc, lamc, rhoc, qc, omc, own_c, 2)
    for x in range(4):
        row = jnp.broadcast_to(st[x : x + 1, :], (8, 8))
        col = jnp.sum(jnp.where(eye, row, 0.0), axis=1, keepdims=True)
        own_f[32 + x] = 1.0 / jnp.broadcast_to(col, (8, LANES))

    def message(out, right):
        def fine(f, ring):
            return own_f[4 * f + (4 - ring if right else ring - 1)]

        for key, (at, rows) in X_AT.items():
            if key[0] == "f":
                out[at : at + rows] = fine(key[1], key[2])
            elif key[0] == "c":
                x = key[2]
                out[at : at + rows] = own_c[2 * key[1] + ((1 if right else 0) if x is None else x)]
        bits = jnp.where(lane == 17, fine(8, 1), fine(8, 2))
        for c in range(3):
            for r in range(2):
                to = 4 * c + 2 * r
                both = jnp.logical_or(lane == to, lane == to + 1)
                bits = jnp.where(both, lane_roll(fine(c, 3 + r), to + 2), bits)
        for f in range(3, 8):
            bits = jnp.where(lane == 9 + f, lane_roll(fine(f, 2), 10 + f), bits)
        at = X_AT["bits"][0]
        out[at : at + 8] = bits

    @pl.when(even)
    def _():
        message(inner, True)
        message(outer, False)

    @pl.when(jnp.logical_not(even))
    def _():
        message(inner, False)
        message(outer, True)


def mid_kernel(own_f, own_c, before, both, after, out2, out1, halo):
    gx, gy = lax.axis_index("gx"), lax.axis_index("gy")
    even_x = lax.rem(gx, 2) == 0
    even_y = lax.rem(gy, 2) == 0
    even_side = jnp.where(even_x, 1, 0)

    @pl.when(inner_before(gx, gy))
    def _():
        halo[even_side] = before[...]

    @pl.when(jnp.logical_not(inner_before(gx, gy)))
    def _():
        halo[even_side] = after[...]

    at_end = jnp.logical_or(gx == 0, gx == lax.axis_size("gx") - 1)

    @pl.when(at_end)
    def _():
        halo[1 - even_side] = jnp.zeros((X_ROWS, LANES), F32)

    @pl.when(jnp.logical_and(even_x, jnp.logical_not(at_end)))
    def _():
        halo[0] = both[0:X_ROWS]

    @pl.when(jnp.logical_not(jnp.logical_or(even_x, at_end)))
    def _():
        halo[1] = both[X_ROWS : 2 * X_ROWS]

    def message(out, up):
        for key, (at, rows) in Y_AT.items():
            fine = (8 - rows if up else 0), (8 if up else rows)
            coarse = (2, 4) if up else (0, 2)
            if key[0] == "bits":
                src = X_AT["bits"][0]
                out[at : at + rows] = halo[key[1], src + fine[0] : src + fine[1]]
                continue
            kind, f, x = key
            wide = 4 if kind == "f" else 2
            part = fine if kind == "f" else coarse
            if 0 <= x < wide:
                out[at : at + rows] = (own_f if kind == "f" else own_c)[wide * f + x, part[0] : part[1]]
            else:
                ring = -x if x < 0 else x - wide + 1
                if kind == "f":
                    src = X_AT["f", f, ring][0]
                else:
                    src = X_AT["c", f, x % 2 if f < 3 else None][0]
                out[at : at + rows] = halo[0 if x < 0 else 1, src + part[0] : src + part[1]]

    @pl.when(even_y)
    def _():
        message(out1, True)
        message(out2, False)

    @pl.when(jnp.logical_not(even_y))
    def _():
        message(out1, False)
        message(out2, True)


def operator(w, zp, zm, x, inv_h2, inv_flat, inv_slant, inv_hz2):
    def dz(c, at):
        return zp[c, at] - zm[c, at]

    def up(tile):
        return row_roll(tile, -1)

    def down(tile):
        return row_roll(tile, 1)

    def dy(c, at):
        return up(w[c, at]) - down(w[c, at])

    dxx = [w[c, x + 1] + w[c, x - 1] - 2.0 * w[c, x] for c in range(3)]
    dyy = [up(w[c, x]) + down(w[c, x]) - 2.0 * w[c, x] for c in range(3)]
    dzz = [zp[c, x] + zm[c, x] - 2.0 * w[c, x] for c in range(3)]
    lap = [(dxx[c] + dyy[c]) * inv_h2 + dzz[c] * inv_hz2 for c in range(3)]
    yz = [up(dz(c, x)) - down(dz(c, x)) for c in (1, 2)]
    grad = [
        dxx[0] * inv_h2 + (dy(1, x + 1) - dy(1, x - 1)) * inv_flat + (dz(2, x + 1) - dz(2, x - 1)) * inv_slant,
        (dy(0, x + 1) - dy(0, x - 1)) * inv_flat + dyy[1] * inv_h2 + yz[1] * inv_slant,
        (dz(0, x + 1) - dz(0, x - 1) + yz[0]) * inv_slant + dzz[2] * inv_hz2,
    ]
    return lap, grad


def post_kernel(
    own_f, own_c, hx, y2, y1, uc, mc, qc, omc, uf, mf, qf, omf, uc_out, uf_out, mc_out, mf_out, hy, ext_f, ext_c, scr
):
    gx, gy = lax.axis_index("gx"), lax.axis_index("gy")
    even_y = lax.rem(gy, 2) == 0

    @pl.when(even_y)
    def _():
        hy[0] = y2[...]
        hy[1] = y1[Y_ROWS : 2 * Y_ROWS]

    @pl.when(jnp.logical_not(even_y))
    def _():
        hy[0] = y1[0:Y_ROWS]
        hy[1] = y2[...]

    index = {}

    def extended(key, own):
        at, rows = Y_AT[key]
        if key[0] == "c":
            ext, tall, far = ext_c, 4, 8
        else:
            ext, tall, far = ext_f, 8, 16
        k = index.setdefault(key, len([i for i in index if (i[0] == "c") == (key[0] == "c")]))
        ext[k, 0:tall] = own
        ext[k, tall : tall + rows] = hy[1, at : at + rows]
        ext[k, far - rows : far] = hy[0, at : at + rows]
        return ext[k]

    def x_rows(side, key):
        at, rows = X_AT[key]
        return hx[side, at : at + rows]

    slots = [0]

    def slot():
        slots[0] += 1
        return slots[0] - 1

    lane_f = lax.broadcasted_iota(jnp.int32, (16, LANES), 1)
    lane_c = lax.broadcasted_iota(jnp.int32, (8, LANES), 1)
    row = lax.broadcasted_iota(jnp.int32, (16, LANES), 0)
    outside_y = jnp.logical_or(
        jnp.logical_and(row >= 12, gy == 0),
        jnp.logical_and(jnp.logical_and(row >= 8, row < 12), gy == lax.axis_size("gy") - 1),
    )
    keep_y = jnp.where(outside_y, 0.0, 1.0).astype(F32)
    keep_left = jnp.where(gx == 0, 0.0, 1.0).astype(F32)
    keep_right = jnp.where(gx == lax.axis_size("gx") - 1, 0.0, 1.0).astype(F32)

    wf, wc, af, ac, cf, cc, rz = {}, {}, {}, {}, {}, {}, {}

    def keep(kind, f, x, own):
        tile = extended((kind, f, x), own)
        if f < 3:
            (wf if kind == "f" else wc)[f, x] = tile
        elif f < 6:
            (af if kind == "f" else ac)[f - 3, x] = tile
        elif f < 8:
            (cf if kind == "f" else cc)[f - 6, x] = tile
        else:
            rz[x] = tile

    for f in range(9):
        for x in range(4):
            keep("f", f, x, own_f[4 * f + x])
    for f in range(8):
        for x in range(2):
            keep("c", f, x, own_c[2 * f + x])
    for side in range(2):

        def col(ring):
            return 3 + ring if side else -ring

        for c in range(3):
            keep("f", c, col(1), x_rows(side, ("f", c, 1)))
            keep("f", c, col(2), x_rows(side, ("f", c, 2)))
            for x in range(2):
                keep("c", c, (2 if side else -2) + x, x_rows(side, ("c", c, x)))
        for f in range(3, 8):
            keep("f", f, col(1), x_rows(side, ("f", f, 1)))
            keep("c", f, 2 if side else -1, x_rows(side, ("c", f, None)))
        bits = extended(("bits", side), x_rows(side, "bits"))
        for c in range(3):
            for r in range(2):
                wf[c, col(3 + r)] = lane_roll(bits, 126 - 4 * c - 2 * r)
            af[c, col(2)] = lane_roll(bits, 115 - c)
        for t in range(2):
            cf[t, col(2)] = lane_roll(bits, 112 - t)
            rz[col(1 + t)] = jnp.broadcast_to(bits[:, 17 + t : 18 + t], (16, LANES))

    def prolong(field, c, x):
        cx = x // 2
        tile = 0.75 * field[c, cx] + 0.25 * field[c, cx + 1 if x % 2 else cx - 1]
        at = slot()
        scr[at, pl.ds(0, 8, stride=2), :] = 0.75 * tile + 0.25 * row_roll(tile, 1)
        scr[at, pl.ds(1, 8, stride=2), :] = 0.75 * tile + 0.25 * row_roll(tile, -1)
        out = scr[at] * keep_y
        return out * keep_left if x < 0 else out * keep_right if x > 3 else out

    def restrict(field, c, cx):
        at = slot()
        scr[at] = field[c, 2 * cx] + field[c, 2 * cx + 1]
        return 0.25 * (scr[at, pl.ds(0, 8, stride=2), :] + scr[at, pl.ds(1, 8, stride=2), :])

    def neighbours(fine, coarse, reach_f, reach_c):
        zp_f, zm_f, zp_c, zm_c = {}, {}, {}, {}
        for c in range(3):
            for x in reach_f:
                tile = fine[c, x]
                zp_f[c, x] = jnp.where(lane_f == LANES - 1, lane_roll(prolong(coarse, c, x), -1), lane_roll(tile, -1))
                zm_f[c, x] = jnp.where(lane_f == 0, tile, lane_roll(tile, 1))
            for x in reach_c:
                tile = coarse[c, x]
                zp_c[c, x] = jnp.where(lane_c == LANES - 1, 0.0, lane_roll(tile, -1))
                zm_c[c, x] = jnp.where(lane_c == 0, lane_roll(restrict(fine, c, x), 1), lane_roll(tile, 1))
        return zp_f, zm_f, zp_c, zm_c

    zp_f, zm_f, zp_c, zm_c = neighbours(wf, wc, range(-3, 7), range(-2, 4))
    wf1, wc1 = {}, {}
    for x in range(-2, 6):
        lap, grad = operator(wf, zp_f, zm_f, x, 4.0, 1.0, 0.5 * rz[x], rz[x] * rz[x])
        for c in range(3):
            wf1[c, x] = af[c, x] + cf[0, x] * lap[c] + cf[1, x] * grad[c]
    for x in range(-1, 3):
        lap, grad = operator(wc, zp_c, zm_c, x, 1.0, 0.25, 0.25, 1.0)
        for c in range(3):
            wc1[c, x] = ac[c, x] + cc[0, x] * lap[c] + cc[1, x] * grad[c]

    zp_f, zm_f, zp_c, zm_c = neighbours(wf1, wc1, range(-1, 5), range(-1, 3))

    def finish(w1, lap, grad, c0, c1, u_r, m_r, q_r, om_r, u_out, m_out, x, tall):
        u = [u_r[c, x] for c in range(3)]
        om = [om_r[l, x] for l in range(3)]
        mem = [[m_r[l, c, x] for c in range(3)] for l in range(3)]
        _, nxt, new = relax(u, mem, [q_r[l, x] for l in range(3)], om)
        for c in range(3):
            u1 = w1[c, x][0:tall] + new[c]
            u_out[c, x] = 2.0 * u1 - u[c] + (c0 * lap[c] + c1 * grad[c])[0:tall]
            for l in range(3):
                m_out[l, c, x] = nxt[l][c] + DT * om[l] * (u1 - nxt[l][c])

    for x in range(4):
        lap, grad = operator(wf1, zp_f, zm_f, x, 4.0, 1.0, 0.5 * rz[x], rz[x] * rz[x])
        finish(wf1, lap, grad, cf[0, x], cf[1, x], uf, mf, qf, omf, uf_out, mf_out, x, 8)
    for x in range(2):
        lap, grad = operator(wc1, zp_c, zm_c, x, 1.0, 0.25, 0.25, 1.0)
        finish(wc1, lap, grad, cc[0, x], cc[1, x], uc, mc, qc, omc, uc_out, mc_out, x, 4)


SCRATCH = 3 * (10 + 6 + 6 + 4)


SEAM = 12


def inner_before(gx, gy):
    return (gx % SEAM < SEAM - 2) | (gy >= -(-5 * lax.axis_size("gy") // 8))


def x_inner(value, before):
    ny = lax.axis_size("gy")
    pairs = []
    for i in range(0, lax.axis_size("gx") - 1, 2):
        for j in range(ny):
            if bool(inner_before(i, j)) == before:
                pairs += [(i * ny + j, (i + 1) * ny + j), ((i + 1) * ny + j, i * ny + j)]
    return lax.ppermute(value, ("gx", "gy"), pairs)


def swap(value, axis, first):
    pairs = []
    for i in range(first, lax.axis_size(axis) - 1, 2):
        pairs += [(i, i + 1), (i + 1, i)]
    return lax.ppermute(value, axis, pairs)


def gather_pairs(value, axis, first):
    nx, ny = lax.axis_size("gx"), lax.axis_size("gy")
    size, other = (nx, ny) if axis == "gx" else (ny, nx)

    def flat(i, k):
        return i * ny + k if axis == "gx" else k * ny + i

    groups = [[flat(i, k), flat(i + 1, k)] for k in range(other) for i in range(first, size - 1, 2)]
    if first:
        groups += [[flat(i, k), flat(i, k + 1)] for i in (0, size - 1) for k in range(0, other, 2)]
    return lax.all_gather(value, ("gx", "gy"), axis_index_groups=sorted(groups), tiled=True)


def call(kernel, shapes, scratch=(), first=False, last=False):
    vmem = pl.BlockSpec(memory_space=pltpu.VMEM)

    def run(*args):
        if not first:
            args = [pltpu.with_memory_space_constraint(a, pltpu.VMEM) for a in args]
        return pl.pallas_call(
            kernel,
            out_shape=[(jax.ShapeDtypeStruct if last else pltpu.VMEM)(s, F32) for s in shapes],
            in_specs=[vmem] * len(args),
            out_specs=[vmem] * len(shapes),
            scratch_shapes=list(scratch),
        )(*args)

    return run


def shards(
    u_now_c,
    u_prev_c,
    memory_c,
    mu_c,
    lam_c,
    rho_c,
    q_c,
    omega_c,
    u_now_f,
    u_prev_f,
    memory_f,
    mu_f,
    lam_f,
    rho_f,
    q_f,
    omega_f,
    stretch_f,
):
    inner, outer, own_f, own_c = call(
        pre_kernel, [(X_ROWS, LANES)] * 2 + [(36, 8, LANES), (16, 4, LANES)], first=True
    )(
        u_now_c, u_prev_c, memory_c, mu_c, lam_c, rho_c, q_c, omega_c,
        u_now_f, u_prev_f, memory_f, mu_f, lam_f, rho_f, q_f, omega_f, stretch_f,
    )
    before = x_inner(inner, True)
    both = gather_pairs(outer, "gx", 1)
    both, inner = lax.optimization_barrier((both, inner))
    after = x_inner(inner, False)
    out2, out1, halo = call(mid_kernel, [(Y_ROWS, LANES)] * 2 + [(2, X_ROWS, LANES)])(own_f, own_c, before, both, after)
    y2 = swap(out2, "gy", 1)
    y1 = gather_pairs(out1, "gy", 0)
    return tuple(
        call(
            post_kernel,
            [u_now_c.shape, u_now_f.shape, memory_c.shape, memory_f.shape],
            [
                pltpu.VMEM((2, Y_ROWS, LANES), F32),
                pltpu.VMEM((len(Y_F), 16, LANES), F32),
                pltpu.VMEM((len(Y_C), 8, LANES), F32),
                pltpu.VMEM((SCRATCH, 16, LANES), F32),
            ],
            last=True,
        )(own_f, own_c, halo, y2, y1, u_now_c, memory_c, q_c, omega_c, u_now_f, memory_f, q_f, omega_f)
    )


def solution(mesh):
    def level(*lead):
        return P(*lead, "gx", "gy", None)

    inputs = (level(None), level(None), level(None, None), level(), level(), level(), level(None), level(None))
    return jax.shard_map(
        shards,
        mesh=mesh,
        in_specs=inputs + inputs + (P("gx", "gy"),),
        out_specs=(level(None), level(None), level(None, None), level(None, None)),
        check_vma=False,
    )
```

profile of v0, /device:TPU:57, one launch (start us, length us, event | category | flops | bytes accessed | tf_op | source)
XLA Modules:
  0.0 37.7 jit_solution(15170568340873598210)
XLA Ops:
  0.6 1.3 %shard_map.192 = (f32[144,128]{1,0:T(8,128)S(1)}, f32[144,128]{1,0:T(8,128)S(1)}, f32[36,8,128]{2,1,0:T(8,128)S(1)}, f32[16,4,128]{2,1,0:T(4,128)S(1)}) custom-call(f32[3,2,4,128]{3,2,1,0:T(4,128)} %uc.3, f32[3,2,4,128]{3,2,1,0:T(4,128)} %pc.1, f32[3,3,2,4,128]{4,3,2,1,0:T(4,128)} %mc.3, f32[2,4,128]{2,1,0:T(4,128)} %muc.1, f32[2,4,128]{2,1,0:T(4,128)} %lamc.1, ...), custom_call_target="tpu_custom_call" | custom-call | tf_op jit(solution)/shard_map/pallas_call | solution.py:395
  1.9 18.0 %all_gather.6.both = f32[288,128]{1,0:T(8,128)S(1)} all-gather(f32[144,128]{1,0:T(8,128)S(1)} %get-tuple-element.16), channel_id=1, replica_groups={{0,1},{2,3},{4,5},{6,7},{8,16},{9,17},{10,18},{11,19},{12,20},{13,21},{..., dimensions={0}, use_global_device_ids=true | all-gather | bytes 221184 | tf_op jit(solution)/shard_map/all_gather | solution.py:386
  20.0 0.7 %collective-permute-start.1 = (f32[144,128]{1,0:T(8,128)S(1)}, f32[144,128]{1,0:T(8,128)S(1)}, u32[]{:S(2)}, u32[]{:S(2)}) collective-permute-start(f32[144,128]{1,0:T(8,128)S(1)} %get-tuple-element.18), channel_id=1, source_target_pairs={{80,88},{88,80},{81,89},{89,81},{82,90},{90,82},{83,91},{91,83},{8... | collective-permute-start | bytes 221192 | tf_op jit(solution)/shard_map/ppermute | solution.py:366
  20.6 1.9 %collective-permute-start = (f32[144,128]{1,0:T(8,128)S(1)}, f32[144,128]{1,0:T(8,128)S(1)}, u32[]{:S(2)}, u32[]{:S(2)}) collective-permute-start(f32[144,128]{1,0:T(8,128)S(1)} %get-tuple-element.18), channel_id=1, source_target_pairs={{0,8},{8,0},{1,9},{9,1},{2,10},{10,2},{3,11},{11,3},{4,12},{12,4},... | collective-permute-start | bytes 221192 | tf_op jit(solution)/shard_map/ppermute | solution.py:366
  22.6 0.0 collective-permute-done.1.after
  22.6 3.2 %collective-permute-done.before = f32[144,128]{1,0:T(8,128)S(1)} collective-permute-done((f32[144,128]{1,0:T(8,128)S(1)}, f32[144,128]{1,0:T(8,128)S(1)}, u32[]{:S(2)}, u32[]{:S(2)}) %collective-permute-start) | collective-permute-done | bytes 73760 | tf_op jit(solution)/shard_map/ppermute | solution.py:366
  25.7 0.1 shard_map.193
  25.8 7.9 %collective-permute-start.2 = (f32[248,128]{1,0:T(8,128)S(1)}, f32[248,128]{1,0:T(8,128)S(1)}, u32[]{:S(2)}, u32[]{:S(2)}) collective-permute-start(f32[248,128]{1,0:T(8,128)S(1)} %get-tuple-element.20), channel_id=1, source_target_pairs={{1,2},{2,1},{3,4},{4,3},{5,6},{6,5},{9,10},{10,9},{11,12},{12,11},... | collective-permute-start | bytes 380936 | tf_op jit(solution)/shard_map/ppermute | solution.py:373
  33.7 0.0 copy-start
  33.8 0.0 copy-start.1
  33.8 0.0 copy-start.2
  33.8 0.0 copy-start.3
  33.8 0.0 copy-start.4
  33.8 0.0 copy-start.5
  33.8 0.0 copy-start.6
  33.8 0.0 copy-start.7
  33.8 2.1 %all_gather.7.y1 = f32[496,128]{1,0:T(8,128)S(1)} all-gather(f32[248,128]{1,0:T(8,128)S(1)} %get-tuple-element.21), channel_id=1, replica_groups={{0,1},{2,3},{4,5},{6,7},{8,9},{10,11},{12,13},{14,15},{16,17},{18,19},{..., dimensions={0}, use_global_device_ids=true | all-gather | bytes 380928 | tf_op jit(solution)/shard_map/all_gather | solution.py:386
  36.0 0.4 collective-permute-done.2.y2
  36.3 0.0 copy-done
  36.3 0.0 copy-done.1
  36.3 0.0 copy-done.2
  36.3 0.0 copy-done.3
  36.4 0.0 copy-done.4
  36.4 0.0 copy-done.5
  36.4 0.0 copy-done.6
  36.4 0.0 copy-done.7
  36.4 1.3 %shard_map.194 = (f32[3,2,4,128]{3,2,1,0:T(4,128)}, f32[3,4,8,128]{3,2,1,0:T(8,128)}, f32[3,3,2,4,128]{4,3,2,1,0:T(4,128)}, f32[3,3,4,8,128]{4,3,2,1,0:T(8,128)}) custom-call(f32[36,8,128]{2,1,0:T(8,128)S(1)} %get-tuple-element.13.own_f, f32[16,4,128]{2,1,0:T(4,128)S(1)} %get-tuple-element.14.own_c, f32[2,144,128]{2,1,0:T(8,128)S(1)} %get-tuple-element.19.hx, ...), custom_call_target="tpu_custom_call" | custom-call | tf_op jit(solution)/shard_map/pallas_call | solution.py:395
Async XLA Ops:
  20.0 2.6 %collective-permute-start.1 = (f32[144,128]{1,0:T(8,128)S(1)}, f32[144,128]{1,0:T(8,128)S(1)}, u32[]{:S(2)}, u32[]{:S(2)}) collective-permute-start(f32[144,128]{1,0:T(8,128)S(1)} %get-tuple-element.18), channel_id=1, source_target_pairs={{80,88},{88,80},{81,89},{89,81},{82,90},{90,82},{83,91},{91,83},{8... | collective-permute-start | bytes 221192 | tf_op jit(solution)/shard_map/ppermute | solution.py:366
  20.6 5.1 %collective-permute-start = (f32[144,128]{1,0:T(8,128)S(1)}, f32[144,128]{1,0:T(8,128)S(1)}, u32[]{:S(2)}, u32[]{:S(2)}) collective-permute-start(f32[144,128]{1,0:T(8,128)S(1)} %get-tuple-element.18), channel_id=1, source_target_pairs={{0,8},{8,0},{1,9},{9,1},{2,10},{10,2},{3,11},{11,3},{4,12},{12,4},... | collective-permute-start | bytes 221192 | tf_op jit(solution)/shard_map/ppermute | solution.py:366
  25.8 10.5 %collective-permute-start.2 = (f32[248,128]{1,0:T(8,128)S(1)}, f32[248,128]{1,0:T(8,128)S(1)}, u32[]{:S(2)}, u32[]{:S(2)}) collective-permute-start(f32[248,128]{1,0:T(8,128)S(1)} %get-tuple-element.20), channel_id=1, source_target_pairs={{1,2},{2,1},{3,4},{4,3},{5,6},{6,5},{9,10},{10,9},{11,12},{12,11},... | collective-permute-start | bytes 380936 | tf_op jit(solution)/shard_map/ppermute | solution.py:373
  33.7 2.6 %copy-start = (f32[3,3,4,8,128]{4,3,2,1,0:T(8,128)S(1)}, f32[3,3,4,8,128]{4,3,2,1,0:T(8,128)}, u32[]{:S(2)}) copy-start(f32[3,3,4,8,128]{4,3,2,1,0:T(8,128)} %mf.3) | copy-start | bytes 442372
  33.8 2.6 %copy-start.1 = (f32[3,4,8,128]{3,2,1,0:T(8,128)S(1)}, f32[3,4,8,128]{3,2,1,0:T(8,128)}, u32[]{:S(2)}) copy-start(f32[3,4,8,128]{3,2,1,0:T(8,128)} %uf.3) | copy-start | bytes 147460
  33.8 2.6 %copy-start.2 = (f32[3,4,8,128]{3,2,1,0:T(8,128)S(1)}, f32[3,4,8,128]{3,2,1,0:T(8,128)}, u32[]{:S(2)}) copy-start(f32[3,4,8,128]{3,2,1,0:T(8,128)} %qf.3) | copy-start | bytes 147460
  33.8 2.6 %copy-start.3 = (f32[3,4,8,128]{3,2,1,0:T(8,128)S(1)}, f32[3,4,8,128]{3,2,1,0:T(8,128)}, u32[]{:S(2)}) copy-start(f32[3,4,8,128]{3,2,1,0:T(8,128)} %omf.3) | copy-start | bytes 147460
  33.8 2.6 %copy-start.4 = (f32[3,3,2,4,128]{4,3,2,1,0:T(4,128)S(1)}, f32[3,3,2,4,128]{4,3,2,1,0:T(4,128)}, u32[]{:S(2)}) copy-start(f32[3,3,2,4,128]{4,3,2,1,0:T(4,128)} %mc.3) | copy-start | bytes 110596
  33.8 2.6 %copy-start.5 = (f32[3,2,4,128]{3,2,1,0:T(4,128)S(1)}, f32[3,2,4,128]{3,2,1,0:T(4,128)}, u32[]{:S(2)}) copy-start(f32[3,2,4,128]{3,2,1,0:T(4,128)} %uc.3) | copy-start | bytes 36868
  33.8 2.6 %copy-start.6 = (f32[3,2,4,128]{3,2,1,0:T(4,128)S(1)}, f32[3,2,4,128]{3,2,1,0:T(4,128)}, u32[]{:S(2)}) copy-start(f32[3,2,4,128]{3,2,1,0:T(4,128)} %qc.3) | copy-start | bytes 36868
  33.8 2.6 %copy-start.7 = (f32[3,2,4,128]{3,2,1,0:T(4,128)S(1)}, f32[3,2,4,128]{3,2,1,0:T(4,128)}, u32[]{:S(2)}) copy-start(f32[3,2,4,128]{3,2,1,0:T(4,128)} %omc.3) | copy-start | bytes 36868
where the time goes:
time: 38.3 us; the launch traced here: 37.7 us
  blocking collectives  20.2 us (53%)
  starting transfers between devices  10.5 us (27%)
  waiting for transfers between devices  3.54 us (9%)
  Pallas kernels  2.72 us (7%)
  between operations  0.79 us (2%)
    all_gather x2, blocking collectives, gather_pairs(): lax.all_gather(value, ('gx', 'gy'), axis_index_groups=sorted(groups), til...  20.2 us
    ppermute x1, starting transfers between devices, swap(): return lax.ppermute(value, axis, pairs)  7.91 us
    ppermute x2, waiting for transfers between devices, x_inner(): return lax.ppermute(value, ('gx', 'gy'), pairs)  3.16 us
    pallas_call x3, Pallas kernels, run(): pl.pallas_call(kernel, out_shape=[(jax.ShapeDtypeStruct if last else pltp...  2.72 us
    ppermute x2, starting transfers between devices, x_inner(): return lax.ppermute(value, ('gx', 'gy'), pairs)  2.57 us
  transfers between devices with their start and end apart: 3, of which 2 were waited for; matrix products, arithmetic and copies ran while one was open for 0% of the time, Pallas kernels for 0%

commit v1 on v0

--- a/solution.py
+++ b/solution.py
@@ -19,14 +19,14 @@
 
 
 X_AT, X_ROWS = layout(
-    [(("f", c, r), 8) for r in (1, 2) for c in range(3)]
-    + [(("f", f, 1), 8) for f in range(3, 8)]
+    [(("f", f, 1), 8) for f in range(8)]
     + [("bits", 8)]
+    + [("edge", 4)]
     + [(("c", c, x), 4) for c in range(3) for x in range(2)]
     + [(("c", f, None), 4) for f in range(3, 8)]
 )
 Y_F = (
-    [(("f", c, x), 4) for c in range(3) for x in range(-2, 6)]
+    [(("f", c, x), 4) for c in range(3) for x in range(-1, 5)]
     + [(("bits", side), 4) for side in range(2)]
     + [(("f", f, x), 2) for f in range(3, 8) for x in range(-1, 5)]
     + [(("f", 8, x), 2) for x in range(4)]
@@ -34,7 +34,8 @@
 Y_C = [(("c", c, x), 2) for c in range(3) for x in range(-2, 4)] + [
     (("c", f, x), 2) for f in range(3, 8) for x in range(-1, 3)
 ]
-Y_AT, Y_ROWS = layout(Y_F + Y_C)
+Y_E = [(("edge", side, c), 1) for side in range(2) for c in range(2)]
+Y_AT, Y_ROWS = layout(Y_F + Y_C + Y_E)
 
 
 def lane_roll(tile, by):
@@ -52,10 +53,12 @@
     return old, nxt, new
 
 
-def pre_kernel(uc, pc, mc, muc, lamc, rhoc, qc, omc, uf, pf, mf, muf, lamf, rhof, qf, omf, st, inner, outer, own_f, own_c):
+def pre_kernel(uc, pc, mc, muc, lamc, rhoc, qc, omc, uf, pf, mf, muf, lamf, rhof, qf, omf, st, inner, outer, own_f, own_c, rows4, rows8):
     even = lax.rem(lax.axis_index("gx"), 2) == 0
     eye = lax.broadcasted_iota(jnp.int32, (8, 8), 0) == lax.broadcasted_iota(jnp.int32, (8, 8), 1)
     lane = lax.broadcasted_iota(jnp.int32, (8, LANES), 1)
+    row = lax.broadcasted_iota(jnp.int32, (8, LANES), 0)
+    rows4[...] = jnp.zeros((3, 8, LANES), F32)
 
     def level(u_r, p_r, m_r, mu_r, lam_r, rho_r, q_r, om_r, own, wide):
         for x in range(wide):
@@ -73,26 +76,55 @@
     level(uf, pf, mf, muf, lamf, rhof, qf, omf, own_f, 4)
     level(uc, pc, mc, muc, lamc, rhoc, qc, omc, own_c, 2)
     for x in range(4):
-        row = jnp.broadcast_to(st[x : x + 1, :], (8, 8))
-        col = jnp.sum(jnp.where(eye, row, 0.0), axis=1, keepdims=True)
+        heights = jnp.broadcast_to(st[x : x + 1, :], (8, 8))
+        col = jnp.sum(jnp.where(eye, heights, 0.0), axis=1, keepdims=True)
         own_f[32 + x] = 1.0 / jnp.broadcast_to(col, (8, LANES))
 
     def message(out, right):
         def fine(f, ring):
             return own_f[4 * f + (4 - ring if right else ring - 1)]
 
+        shear, lame = fine(6, 1), fine(7, 1)
+        sign = -1.0 if right else 1.0
+        slant = 0.5 * fine(8, 1)
+        ring2 = [fine(c, 2) for c in range(3)]
+
+        def dy(tile):
+            return jnp.where(row == 7, 0.0, row_roll(tile, -1)) - jnp.where(row == 0, 0.0, row_roll(tile, 1))
+
+        def dz(c):
+            far, close = (own_c[2 * c], own_c[2 * c + 1]) if right else (own_c[2 * c + 1], own_c[2 * c])
+            plane, ghost = rows4.at[c], rows8.at[c]
+            plane[1:5] = 0.75 * close + 0.25 * far
+            ghost[pl.ds(0, 4, stride=2), :] = 0.75 * plane[1:5] + 0.25 * plane[0:4]
+            ghost[pl.ds(1, 4, stride=2), :] = 0.75 * plane[1:5] + 0.25 * plane[2:6]
+            tile = ring2[c]
+            above = jnp.where(lane == LANES - 1, lane_roll(ghost[...], -1), lane_roll(tile, -1))
+            return above - jnp.where(lane == 0, tile, lane_roll(tile, 1))
+
+        extra = [
+            4.0 * ring2[0] + sign * (dy(ring2[1]) + dz(2) * slant),
+            sign * dy(ring2[0]),
+            sign * dz(0) * slant,
+        ]
         for key, (at, rows) in X_AT.items():
-            if key[0] == "f":
-                out[at : at + rows] = fine(key[1], key[2])
+            if key[0] == "f" and 3 <= key[1] < 6:
+                c = key[1] - 3
+                out[at : at + rows] = fine(key[1], 1) + shear * (4.0 * ring2[c]) + lame * extra[c]
+            elif key[0] == "f":
+                out[at : at + rows] = fine(key[1], 1)
             elif key[0] == "c":
                 x = key[2]
                 out[at : at + rows] = own_c[2 * key[1] + ((1 if right else 0) if x is None else x)]
+        at = X_AT["edge"][0]
+        for c in range(2):
+            for k, y in enumerate((0, 7)):
+                out[at + 2 * c + k : at + 2 * c + k + 1] = own_f[4 * c + (2 if right else 1), y : y + 1]
         bits = jnp.where(lane == 17, fine(8, 1), fine(8, 2))
         for c in range(3):
-            for r in range(2):
-                to = 4 * c + 2 * r
+            for ring, to in ((2, 19 + 2 * c), (3, 4 * c), (4, 4 * c + 2)):
                 both = jnp.logical_or(lane == to, lane == to + 1)
-                bits = jnp.where(both, lane_roll(fine(c, 3 + r), to + 2), bits)
+                bits = jnp.where(both, lane_roll(fine(c, ring), to + 2), bits)
         for f in range(3, 8):
             bits = jnp.where(lane == 9 + f, lane_roll(fine(f, 2), 10 + f), bits)
         at = X_AT["bits"][0]
@@ -144,6 +176,10 @@
             if key[0] == "bits":
                 src = X_AT["bits"][0]
                 out[at : at + rows] = halo[key[1], src + fine[0] : src + fine[1]]
+                continue
+            if key[0] == "edge":
+                src = X_AT["edge"][0] + 2 * key[2] + (1 if up else 0)
+                out[at : at + 1] = halo[key[1], src : src + 1]
                 continue
             kind, f, x = key
             wide = 4 if kind == "f" else 2
@@ -169,9 +205,14 @@
         message(out2, True)
 
 
-def operator(w, zp, zm, x, inv_h2, inv_flat, inv_slant, inv_hz2):
+def operator(w, zp, zm, x, inv_h2, inv_flat, inv_slant, inv_hz2, given=(None, None, None)):
+    given_at, given_dy, given_dz = given
+
+    def wx(c, at):
+        return 0.0 if at == given_at else w[c, at]
+
     def dz(c, at):
-        return zp[c, at] - zm[c, at]
+        return given_dz[c] if at == given_at else zp[c, at] - zm[c, at]
 
     def up(tile):
         return row_roll(tile, -1)
@@ -180,9 +221,9 @@
         return row_roll(tile, 1)
 
     def dy(c, at):
-        return up(w[c, at]) - down(w[c, at])
-
-    dxx = [w[c, x + 1] + w[c, x - 1] - 2.0 * w[c, x] for c in range(3)]
+        return given_dy[c] if at == given_at else up(w[c, at]) - down(w[c, at])
+
+    dxx = [wx(c, x + 1) + wx(c, x - 1) - 2.0 * w[c, x] for c in range(3)]
     dyy = [up(w[c, x]) + down(w[c, x]) - 2.0 * w[c, x] for c in range(3)]
     dzz = [zp[c, x] + zm[c, x] - 2.0 * w[c, x] for c in range(3)]
     lap = [(dxx[c] + dyy[c]) * inv_h2 + dzz[c] * inv_hz2 for c in range(3)]
@@ -196,7 +237,7 @@
 
 
 def post_kernel(
-    own_f, own_c, hx, y2, y1, uc, mc, qc, omc, uf, mf, qf, omf, uc_out, uf_out, mc_out, mf_out, hy, ext_f, ext_c, scr
+    own_f, own_c, hx, y2, y1, uc, mc, qc, omc, uf, mf, qf, omf, uc_out, uf_out, mc_out, mf_out, hy, ext_f, ext_c, ext_e, scr
 ):
     gx, gy = lax.axis_index("gx"), lax.axis_index("gy")
     even_y = lax.rem(gy, 2) == 0
@@ -272,7 +313,6 @@
 
         for c in range(3):
             keep("f", c, col(1), x_rows(side, ("f", c, 1)))
-            keep("f", c, col(2), x_rows(side, ("f", c, 2)))
             for x in range(2):
                 keep("c", c, (2 if side else -2) + x, x_rows(side, ("c", c, x)))
         for f in range(3, 8):
@@ -282,6 +322,7 @@
         for c in range(3):
             for r in range(2):
                 wf[c, col(3 + r)] = lane_roll(bits, 126 - 4 * c - 2 * r)
+            wf[c, col(2)] = lane_roll(bits, 107 - 2 * c)
             af[c, col(2)] = lane_roll(bits, 115 - c)
         for t in range(2):
             cf[t, col(2)] = lane_roll(bits, 112 - t)
@@ -295,6 +336,28 @@
         scr[at, pl.ds(1, 8, stride=2), :] = 0.75 * tile + 0.25 * row_roll(tile, -1)
         out = scr[at] * keep_y
         return out * keep_left if x < 0 else out * keep_right if x > 3 else out
+
+    crosses = (row == 0) | (row == 7) | (row == 8) | (row == 15)
+    across = []
+    for side in range(2):
+        given_dy, given_dz = {}, {}
+        for c in range(2):
+            k = 2 * side + c
+            src, at = X_AT["edge"][0] + 2 * c, Y_AT["edge", side, c][0]
+            ext_e[k] = jnp.zeros((16, LANES), F32)
+            ext_e[k, 0:1] = hx[side, src : src + 1]
+            ext_e[k, 7:8] = hx[side, src + 1 : src + 2]
+            ext_e[k, 8:9] = hy[1, at : at + 1]
+            ext_e[k, 15:16] = hy[0, at : at + 1]
+            tile = ext_e[k]
+            given_dy[c] = jnp.where(crosses, row_roll(tile, -1) - row_roll(tile, 1), 0.0)
+        for c in (0, 2):
+            tile = 0.75 * wc[c, 2 if side else -1] + 0.25 * wc[c, 3 if side else -2]
+            at = slot()
+            scr[at, pl.ds(0, 8, stride=2), :] = 0.25 * row_roll(tile, 1)
+            scr[at, pl.ds(1, 8, stride=2), :] = 0.25 * row_roll(tile, -1)
+            given_dz[c] = jnp.where(crosses & (lane_f == LANES - 1), lane_roll(scr[at], -1), 0.0)
+        across.append((5 if side else -2, given_dy, given_dz))
 
     def restrict(field, c, cx):
         at = slot()
@@ -317,7 +380,8 @@
     zp_f, zm_f, zp_c, zm_c = neighbours(wf, wc, range(-3, 7), range(-2, 4))
     wf1, wc1 = {}, {}
     for x in range(-2, 6):
-        lap, grad = operator(wf, zp_f, zm_f, x, 4.0, 1.0, 0.5 * rz[x], rz[x] * rz[x])
+        given = {-1: across[0], 4: across[1]}.get(x, (None, None, None))
+        lap, grad = operator(wf, zp_f, zm_f, x, 4.0, 1.0, 0.5 * rz[x], rz[x] * rz[x], given)
         for c in range(3):
             wf1[c, x] = af[c, x] + cf[0, x] * lap[c] + cf[1, x] * grad[c]
     for x in range(-1, 3):
@@ -346,7 +410,7 @@
         finish(wc1, lap, grad, cc[0, x], cc[1, x], uc, mc, qc, omc, uc_out, mc_out, x, 4)
 
 
-SCRATCH = 3 * (10 + 6 + 6 + 4)
+SCRATCH = 3 * (10 + 6 + 6 + 4) + 4
 
 
 SEAM = 12
@@ -423,7 +487,10 @@
     stretch_f,
 ):
     inner, outer, own_f, own_c = call(
-        pre_kernel, [(X_ROWS, LANES)] * 2 + [(36, 8, LANES), (16, 4, LANES)], first=True
+        pre_kernel,
+        [(X_ROWS, LANES)] * 2 + [(36, 8, LANES), (16, 4, LANES)],
+        [pltpu.VMEM((3, 8, LANES), F32), pltpu.VMEM((3, 8, LANES), F32)],
+        first=True,
     )(
         u_now_c, u_prev_c, memory_c, mu_c, lam_c, rho_c, q_c, omega_c,
         u_now_f, u_prev_f, memory_f, mu_f, lam_f, rho_f, q_f, omega_f, stretch_f,
@@ -443,6 +510,7 @@
                 pltpu.VMEM((2, Y_ROWS, LANES), F32),
                 pltpu.VMEM((len(Y_F), 16, LANES), F32),
                 pltpu.VMEM((len(Y_C), 8, LANES), F32),
+                pltpu.VMEM((4, 16, LANES), F32),
                 pltpu.VMEM((SCRATCH, 16, LANES), F32),
             ],
             last=True,

time: 38.3 us -> 37.2 us (0.971)
  starting transfers between devices: 10.5 us -> 10 us
    ppermute x1, starting transfers between devices: 7.91 us -> 7.45 us  [swap(): return lax.ppermute(value, axis, pairs)]
where the time goes in v1:
time: 37.2 us; the launch traced here: 36.9 us
  blocking collectives  20 us (54%)
  starting transfers between devices  10 us (27%)
  waiting for transfers between devices  3.34 us (9%)
  Pallas kernels  2.8 us (8%)
  between operations  0.78 us (2%)
    all_gather x2, blocking collectives, gather_pairs(): lax.all_gather(value, ('gx', 'gy'), axis_index_groups=sorted(groups), til...  20 us
    ppermute x1, starting transfers between devices, swap(): return lax.ppermute(value, axis, pairs)  7.45 us
    ppermute x2, waiting for transfers between devices, x_inner(): return lax.ppermute(value, ('gx', 'gy'), pairs)  3.03 us
    pallas_call x3, Pallas kernels, run(): pl.pallas_call(kernel, out_shape=[(jax.ShapeDtypeStruct if last else pltp...  2.8 us
    ppermute x2, starting transfers between devices, x_inner(): return lax.ppermute(value, ('gx', 'gy'), pairs)  2.57 us
  transfers between devices with their start and end apart: 3, of which 2 were waited for; matrix products, arithmetic and copies ran while one was open for 0% of the time, Pallas kernels for 0%

profile of v1, /device:TPU:57, one launch (start us, length us, event | category | flops | bytes accessed | tf_op | source)
XLA Modules:
  0.0 36.9 jit_solution(8414982171585009104)
XLA Ops:
  0.6 1.3 %shard_map.192 = (f32[120,128]{1,0:T(8,128)S(1)}, f32[120,128]{1,0:T(8,128)S(1)}, f32[36,8,128]{2,1,0:T(8,128)S(1)}, f32[16,4,128]{2,1,0:T(4,128)S(1)}) custom-call(f32[3,2,4,128]{3,2,1,0:T(4,128)} %uc.3, f32[3,2,4,128]{3,2,1,0:T(4,128)} %pc.1, f32[3,3,2,4,128]{4,3,2,1,0:T(4,128)} %mc.3, f32[2,4,128]{2,1,0:T(4,128)} %muc.1, f32[2,4,128]{2,1,0:T(4,128)} %lamc.1, ...), custom_call_target="tpu_custom_call" | custom-call | tf_op jit(solution)/shard_map/pallas_call | solution.py:459
  2.0 17.8 %all_gather.6.both = f32[240,128]{1,0:T(8,128)S(1)} all-gather(f32[120,128]{1,0:T(8,128)S(1)} %get-tuple-element.16), channel_id=1, replica_groups={{0,1},{2,3},{4,5},{6,7},{8,16},{9,17},{10,18},{11,19},{12,20},{13,21},{..., dimensions={0}, use_global_device_ids=true | all-gather | bytes 184320 | tf_op jit(solution)/shard_map/all_gather | solution.py:450
  19.8 0.7 %collective-permute-start.1 = (f32[120,128]{1,0:T(8,128)S(1)}, f32[120,128]{1,0:T(8,128)S(1)}, u32[]{:S(2)}, u32[]{:S(2)}) collective-permute-start(f32[120,128]{1,0:T(8,128)S(1)} %get-tuple-element.18), channel_id=1, source_target_pairs={{80,88},{88,80},{81,89},{89,81},{82,90},{90,82},{83,91},{91,83},{8... | collective-permute-start | bytes 184328 | tf_op jit(solution)/shard_map/ppermute | solution.py:430
  20.5 1.9 %collective-permute-start = (f32[120,128]{1,0:T(8,128)S(1)}, f32[120,128]{1,0:T(8,128)S(1)}, u32[]{:S(2)}, u32[]{:S(2)}) collective-permute-start(f32[120,128]{1,0:T(8,128)S(1)} %get-tuple-element.18), channel_id=1, source_target_pairs={{0,8},{8,0},{1,9},{9,1},{2,10},{10,2},{3,11},{11,3},{4,12},{12,4},... | collective-permute-start | bytes 184328 | tf_op jit(solution)/shard_map/ppermute | solution.py:430
  22.4 0.0 collective-permute-done.1.after
  22.4 3.0 %collective-permute-done.before = f32[120,128]{1,0:T(8,128)S(1)} collective-permute-done((f32[120,128]{1,0:T(8,128)S(1)}, f32[120,128]{1,0:T(8,128)S(1)}, u32[]{:S(2)}, u32[]{:S(2)}) %collective-permute-start) | collective-permute-done | bytes 61472 | tf_op jit(solution)/shard_map/ppermute | solution.py:430
  25.4 0.0 copy-start.7
  25.4 0.1 shard_map.193
  25.5 7.4 %collective-permute-start.2 = (f32[232,128]{1,0:T(8,128)S(1)}, f32[232,128]{1,0:T(8,128)S(1)}, u32[]{:S(2)}, u32[]{:S(2)}) collective-permute-start(f32[232,128]{1,0:T(8,128)S(1)} %get-tuple-element.20), channel_id=1, source_target_pairs={{1,2},{2,1},{3,4},{4,3},{5,6},{6,5},{9,10},{10,9},{11,12},{12,11},... | collective-permute-start | bytes 356360 | tf_op jit(solution)/shard_map/ppermute | solution.py:437
  33.0 0.0 copy-start
  33.0 0.0 copy-start.1
  33.0 0.0 copy-start.2
  33.0 0.0 copy-start.3
  33.1 0.0 copy-start.4
  33.1 0.0 copy-start.5
  33.1 0.0 copy-start.6
  33.1 2.1 %all_gather.7.y1 = f32[464,128]{1,0:T(8,128)S(1)} all-gather(f32[232,128]{1,0:T(8,128)S(1)} %get-tuple-element.21), channel_id=1, replica_groups={{0,1},{2,3},{4,5},{6,7},{8,9},{10,11},{12,13},{14,15},{16,17},{18,19},{..., dimensions={0}, use_global_device_ids=true | all-gather | bytes 356352 | tf_op jit(solution)/shard_map/all_gather | solution.py:450
  35.2 0.3 collective-permute-done.2.y2
  35.5 0.0 copy-done.7
  35.5 0.0 copy-done
  35.5 0.0 copy-done.1
  35.5 0.0 copy-done.2
  35.5 0.0 copy-done.3
  35.5 0.0 copy-done.4
  35.6 0.0 copy-done.5
  35.6 0.0 copy-done.6
  35.6 1.4 %shard_map.194 = (f32[3,2,4,128]{3,2,1,0:T(4,128)}, f32[3,4,8,128]{3,2,1,0:T(8,128)}, f32[3,3,2,4,128]{4,3,2,1,0:T(4,128)}, f32[3,3,4,8,128]{4,3,2,1,0:T(8,128)}) custom-call(f32[36,8,128]{2,1,0:T(8,128)S(1)} %get-tuple-element.13.own_f, f32[16,4,128]{2,1,0:T(4,128)S(1)} %get-tuple-element.14.own_c, f32[2,120,128]{2,1,0:T(8,128)S(1)} %get-tuple-element.19.hx, ...), custom_call_target="tpu_custom_call" | custom-call | tf_op jit(solution)/shard_map/pallas_call | solution.py:459
Async XLA Ops:
  19.8 2.6 %collective-permute-start.1 = (f32[120,128]{1,0:T(8,128)S(1)}, f32[120,128]{1,0:T(8,128)S(1)}, u32[]{:S(2)}, u32[]{:S(2)}) collective-permute-start(f32[120,128]{1,0:T(8,128)S(1)} %get-tuple-element.18), channel_id=1, source_target_pairs={{80,88},{88,80},{81,89},{89,81},{82,90},{90,82},{83,91},{91,83},{8... | collective-permute-start | bytes 184328 | tf_op jit(solution)/shard_map/ppermute | solution.py:430
  20.5 5.0 %collective-permute-start = (f32[120,128]{1,0:T(8,128)S(1)}, f32[120,128]{1,0:T(8,128)S(1)}, u32[]{:S(2)}, u32[]{:S(2)}) collective-permute-start(f32[120,128]{1,0:T(8,128)S(1)} %get-tuple-element.18), channel_id=1, source_target_pairs={{0,8},{8,0},{1,9},{9,1},{2,10},{10,2},{3,11},{11,3},{4,12},{12,4},... | collective-permute-start | bytes 184328 | tf_op jit(solution)/shard_map/ppermute | solution.py:430
  25.4 10.1 %copy-start.7 = (f32[3,2,4,128]{3,2,1,0:T(4,128)S(1)}, f32[3,2,4,128]{3,2,1,0:T(4,128)}, u32[]{:S(2)}) copy-start(f32[3,2,4,128]{3,2,1,0:T(4,128)} %omc.3) | copy-start | bytes 36868
  25.5 10.0 %collective-permute-start.2 = (f32[232,128]{1,0:T(8,128)S(1)}, f32[232,128]{1,0:T(8,128)S(1)}, u32[]{:S(2)}, u32[]{:S(2)}) collective-permute-start(f32[232,128]{1,0:T(8,128)S(1)} %get-tuple-element.20), channel_id=1, source_target_pairs={{1,2},{2,1},{3,4},{4,3},{5,6},{6,5},{9,10},{10,9},{11,12},{12,11},... | collective-permute-start | bytes 356360 | tf_op jit(solution)/shard_map/ppermute | solution.py:437
  33.0 2.5 %copy-start = (f32[3,3,4,8,128]{4,3,2,1,0:T(8,128)S(1)}, f32[3,3,4,8,128]{4,3,2,1,0:T(8,128)}, u32[]{:S(2)}) copy-start(f32[3,3,4,8,128]{4,3,2,1,0:T(8,128)} %mf.3) | copy-start | bytes 442372
  33.0 2.5 %copy-start.1 = (f32[3,4,8,128]{3,2,1,0:T(8,128)S(1)}, f32[3,4,8,128]{3,2,1,0:T(8,128)}, u32[]{:S(2)}) copy-start(f32[3,4,8,128]{3,2,1,0:T(8,128)} %uf.3) | copy-start | bytes 147460
  33.0 2.5 %copy-start.2 = (f32[3,4,8,128]{3,2,1,0:T(8,128)S(1)}, f32[3,4,8,128]{3,2,1,0:T(8,128)}, u32[]{:S(2)}) copy-start(f32[3,4,8,128]{3,2,1,0:T(8,128)} %qf.3) | copy-start | bytes 147460
  33.0 2.5 %copy-start.3 = (f32[3,4,8,128]{3,2,1,0:T(8,128)S(1)}, f32[3,4,8,128]{3,2,1,0:T(8,128)}, u32[]{:S(2)}) copy-start(f32[3,4,8,128]{3,2,1,0:T(8,128)} %omf.3) | copy-start | bytes 147460
  33.1 2.5 %copy-start.4 = (f32[3,3,2,4,128]{4,3,2,1,0:T(4,128)S(1)}, f32[3,3,2,4,128]{4,3,2,1,0:T(4,128)}, u32[]{:S(2)}) copy-start(f32[3,3,2,4,128]{4,3,2,1,0:T(4,128)} %mc.3) | copy-start | bytes 110596
  33.1 2.5 %copy-start.5 = (f32[3,2,4,128]{3,2,1,0:T(4,128)S(1)}, f32[3,2,4,128]{3,2,1,0:T(4,128)}, u32[]{:S(2)}) copy-start(f32[3,2,4,128]{3,2,1,0:T(4,128)} %uc.3) | copy-start | bytes 36868
  33.1 2.5 %copy-start.6 = (f32[3,2,4,128]{3,2,1,0:T(4,128)S(1)}, f32[3,2,4,128]{3,2,1,0:T(4,128)}, u32[]{:S(2)}) copy-start(f32[3,2,4,128]{3,2,1,0:T(4,128)} %qc.3) | copy-start | bytes 36868

commit v2 on v1

--- a/solution.py
+++ b/solution.py
@@ -32,7 +32,7 @@
     + [(("f", 8, x), 2) for x in range(4)]
 )
 Y_C = [(("c", c, x), 2) for c in range(3) for x in range(-2, 4)] + [
-    (("c", f, x), 2) for f in range(3, 8) for x in range(-1, 3)
+    (("c", f, x), 1) for f in range(3, 8) for x in range(-1, 3)
 ]
 Y_E = [(("edge", side, c), 1) for side in range(2) for c in range(2)]
 Y_AT, Y_ROWS = layout(Y_F + Y_C + Y_E)
@@ -172,7 +172,7 @@
     def message(out, up):
         for key, (at, rows) in Y_AT.items():
             fine = (8 - rows if up else 0), (8 if up else rows)
-            coarse = (2, 4) if up else (0, 2)
+            coarse = (4 - rows if up else 0), (4 if up else rows)
             if key[0] == "bits":
                 src = X_AT["bits"][0]
                 out[at : at + rows] = halo[key[1], src + fine[0] : src + fine[1]]
@@ -417,7 +417,7 @@
 
 
 def inner_before(gx, gy):
-    return (gx % SEAM < SEAM - 2) | (gy >= -(-5 * lax.axis_size("gy") // 8))
+    return (gx % SEAM < SEAM - 2) | ((gy >= -(-5 * lax.axis_size("gy") // 8)) & (gy % 2 == 1))
 
 
 def x_inner(value, before):

time: 37.2 us -> 37 us (level)
  no operation moved by 1% of the time
where the time goes in v2:
time: 37 us; the launch traced here: 36.8 us
  blocking collectives  19.9 us (54%)
  starting transfers between devices  10 us (27%)
  waiting for transfers between devices  3.24 us (9%)
  Pallas kernels  2.79 us (8%)
  between operations  0.78 us (2%)
    all_gather x2, blocking collectives, gather_pairs(): lax.all_gather(value, ('gx', 'gy'), axis_index_groups=sorted(groups), til...  19.9 us
    ppermute x1, starting transfers between devices, swap(): return lax.ppermute(value, axis, pairs)  7.45 us
    ppermute x2, waiting for transfers between devices, x_inner(): return lax.ppermute(value, ('gx', 'gy'), pairs)  3.03 us
    pallas_call x3, Pallas kernels, run(): pl.pallas_call(kernel, out_shape=[(jax.ShapeDtypeStruct if last else pltp...  2.79 us
    ppermute x2, starting transfers between devices, x_inner(): return lax.ppermute(value, ('gx', 'gy'), pairs)  2.57 us
  transfers between devices with their start and end apart: 3, of which 2 were waited for; matrix products, arithmetic and copies ran while one was open for 0% of the time, Pallas kernels for 0%

profile of v2, /device:TPU:57, one launch (start us, length us, event | category | flops | bytes accessed | tf_op | source)
XLA Modules:
  0.0 36.8 jit_solution(5741931624451973777)
XLA Ops:
  0.6 1.3 %shard_map.192 = (f32[120,128]{1,0:T(8,128)S(1)}, f32[120,128]{1,0:T(8,128)S(1)}, f32[36,8,128]{2,1,0:T(8,128)S(1)}, f32[16,4,128]{2,1,0:T(4,128)S(1)}) custom-call(f32[3,2,4,128]{3,2,1,0:T(4,128)} %uc.3, f32[3,2,4,128]{3,2,1,0:T(4,128)} %pc.1, f32[3,3,2,4,128]{4,3,2,1,0:T(4,128)} %mc.3, f32[2,4,128]{2,1,0:T(4,128)} %muc.1, f32[2,4,128]{2,1,0:T(4,128)} %lamc.1, ...), custom_call_target="tpu_custom_call" | custom-call | tf_op jit(solution)/shard_map/pallas_call | solution.py:459
  2.0 17.8 %all_gather.6.both = f32[240,128]{1,0:T(8,128)S(1)} all-gather(f32[120,128]{1,0:T(8,128)S(1)} %get-tuple-element.16), channel_id=1, replica_groups={{0,1},{2,3},{4,5},{6,7},{8,16},{9,17},{10,18},{11,19},{12,20},{13,21},{..., dimensions={0}, use_global_device_ids=true | all-gather | bytes 184320 | tf_op jit(solution)/shard_map/all_gather | solution.py:450
  19.8 0.7 %collective-permute-start.1 = (f32[120,128]{1,0:T(8,128)S(1)}, f32[120,128]{1,0:T(8,128)S(1)}, u32[]{:S(2)}, u32[]{:S(2)}) collective-permute-start(f32[120,128]{1,0:T(8,128)S(1)} %get-tuple-element.18), channel_id=1, source_target_pairs={{80,88},{88,80},{81,89},{89,81},{82,90},{90,82},{83,91},{91,83},{8... | collective-permute-start | bytes 184328 | tf_op jit(solution)/shard_map/ppermute | solution.py:430
  20.5 1.9 %collective-permute-start = (f32[120,128]{1,0:T(8,128)S(1)}, f32[120,128]{1,0:T(8,128)S(1)}, u32[]{:S(2)}, u32[]{:S(2)}) collective-permute-start(f32[120,128]{1,0:T(8,128)S(1)} %get-tuple-element.18), channel_id=1, source_target_pairs={{0,8},{8,0},{1,9},{9,1},{2,10},{10,2},{3,11},{11,3},{4,12},{12,4},... | collective-permute-start | bytes 184328 | tf_op jit(solution)/shard_map/ppermute | solution.py:430
  22.4 0.0 collective-permute-done.1.after
  22.4 3.0 %collective-permute-done.before = f32[120,128]{1,0:T(8,128)S(1)} collective-permute-done((f32[120,128]{1,0:T(8,128)S(1)}, f32[120,128]{1,0:T(8,128)S(1)}, u32[]{:S(2)}, u32[]{:S(2)}) %collective-permute-start) | collective-permute-done | bytes 61472 | tf_op jit(solution)/shard_map/ppermute | solution.py:430
  25.4 0.0 copy-start.4
  25.4 0.0 copy-start.7
  25.4 0.1 shard_map.193
  25.6 7.4 %collective-permute-start.2 = (f32[208,128]{1,0:T(8,128)S(1)}, f32[208,128]{1,0:T(8,128)S(1)}, u32[]{:S(2)}, u32[]{:S(2)}) collective-permute-start(f32[208,128]{1,0:T(8,128)S(1)} %get-tuple-element.20), channel_id=1, source_target_pairs={{1,2},{2,1},{3,4},{4,3},{5,6},{6,5},{9,10},{10,9},{11,12},{12,11},... | collective-permute-start | bytes 319496 | tf_op jit(solution)/shard_map/ppermute | solution.py:437
  33.0 0.0 copy-start
  33.0 0.0 copy-start.1
  33.0 0.0 copy-start.2
  33.0 0.0 copy-start.3
  33.1 0.0 copy-start.5
  33.1 0.0 copy-start.6
  33.1 2.1 %all_gather.7.y1 = f32[416,128]{1,0:T(8,128)S(1)} all-gather(f32[208,128]{1,0:T(8,128)S(1)} %get-tuple-element.21), channel_id=1, replica_groups={{0,1},{2,3},{4,5},{6,7},{8,9},{10,11},{12,13},{14,15},{16,17},{18,19},{..., dimensions={0}, use_global_device_ids=true | all-gather | bytes 319488 | tf_op jit(solution)/shard_map/all_gather | solution.py:450
  35.2 0.2 collective-permute-done.2.y2
  35.4 0.0 copy-done.4
  35.4 0.0 copy-done.7
  35.4 0.0 copy-done
  35.4 0.0 copy-done.1
  35.4 0.0 copy-done.2
  35.4 0.0 copy-done.3
  35.4 0.0 copy-done.5
  35.4 0.0 copy-done.6
  35.4 1.4 %shard_map.194 = (f32[3,2,4,128]{3,2,1,0:T(4,128)}, f32[3,4,8,128]{3,2,1,0:T(8,128)}, f32[3,3,2,4,128]{4,3,2,1,0:T(4,128)}, f32[3,3,4,8,128]{4,3,2,1,0:T(8,128)}) custom-call(f32[36,8,128]{2,1,0:T(8,128)S(1)} %get-tuple-element.13.own_f, f32[16,4,128]{2,1,0:T(4,128)S(1)} %get-tuple-element.14.own_c, f32[2,120,128]{2,1,0:T(8,128)S(1)} %get-tuple-element.19.hx, ...), custom_call_target="tpu_custom_call" | custom-call | tf_op jit(solution)/shard_map/pallas_call | solution.py:459
Async XLA Ops:
  19.8 2.6 %collective-permute-start.1 = (f32[120,128]{1,0:T(8,128)S(1)}, f32[120,128]{1,0:T(8,128)S(1)}, u32[]{:S(2)}, u32[]{:S(2)}) collective-permute-start(f32[120,128]{1,0:T(8,128)S(1)} %get-tuple-element.18), channel_id=1, source_target_pairs={{80,88},{88,80},{81,89},{89,81},{82,90},{90,82},{83,91},{91,83},{8... | collective-permute-start | bytes 184328 | tf_op jit(solution)/shard_map/ppermute | solution.py:430
  20.5 5.0 %collective-permute-start = (f32[120,128]{1,0:T(8,128)S(1)}, f32[120,128]{1,0:T(8,128)S(1)}, u32[]{:S(2)}, u32[]{:S(2)}) collective-permute-start(f32[120,128]{1,0:T(8,128)S(1)} %get-tuple-element.18), channel_id=1, source_target_pairs={{0,8},{8,0},{1,9},{9,1},{2,10},{10,2},{3,11},{11,3},{4,12},{12,4},... | collective-permute-start | bytes 184328 | tf_op jit(solution)/shard_map/ppermute | solution.py:430
  25.4 9.9 %copy-start.4 = (f32[3,3,2,4,128]{4,3,2,1,0:T(4,128)S(1)}, f32[3,3,2,4,128]{4,3,2,1,0:T(4,128)}, u32[]{:S(2)}) copy-start(f32[3,3,2,4,128]{4,3,2,1,0:T(4,128)} %mc.3) | copy-start | bytes 110596
  25.4 9.9 %copy-start.7 = (f32[3,2,4,128]{3,2,1,0:T(4,128)S(1)}, f32[3,2,4,128]{3,2,1,0:T(4,128)}, u32[]{:S(2)}) copy-start(f32[3,2,4,128]{3,2,1,0:T(4,128)} %omc.3) | copy-start | bytes 36868
  25.6 9.8 %collective-permute-start.2 = (f32[208,128]{1,0:T(8,128)S(1)}, f32[208,128]{1,0:T(8,128)S(1)}, u32[]{:S(2)}, u32[]{:S(2)}) collective-permute-start(f32[208,128]{1,0:T(8,128)S(1)} %get-tuple-element.20), channel_id=1, source_target_pairs={{1,2},{2,1},{3,4},{4,3},{5,6},{6,5},{9,10},{10,9},{11,12},{12,11},... | collective-permute-start | bytes 319496 | tf_op jit(solution)/shard_map/ppermute | solution.py:437
  33.0 2.4 %copy-start = (f32[3,3,4,8,128]{4,3,2,1,0:T(8,128)S(1)}, f32[3,3,4,8,128]{4,3,2,1,0:T(8,128)}, u32[]{:S(2)}) copy-start(f32[3,3,4,8,128]{4,3,2,1,0:T(8,128)} %mf.3) | copy-start | bytes 442372
  33.0 2.4 %copy-start.1 = (f32[3,4,8,128]{3,2,1,0:T(8,128)S(1)}, f32[3,4,8,128]{3,2,1,0:T(8,128)}, u32[]{:S(2)}) copy-start(f32[3,4,8,128]{3,2,1,0:T(8,128)} %uf.3) | copy-start | bytes 147460
  33.0 2.4 %copy-start.2 = (f32[3,4,8,128]{3,2,1,0:T(8,128)S(1)}, f32[3,4,8,128]{3,2,1,0:T(8,128)}, u32[]{:S(2)}) copy-start(f32[3,4,8,128]{3,2,1,0:T(8,128)} %qf.3) | copy-start | bytes 147460
  33.0 2.4 %copy-start.3 = (f32[3,4,8,128]{3,2,1,0:T(8,128)S(1)}, f32[3,4,8,128]{3,2,1,0:T(8,128)}, u32[]{:S(2)}) copy-start(f32[3,4,8,128]{3,2,1,0:T(8,128)} %omf.3) | copy-start | bytes 147460
  33.1 2.4 %copy-start.5 = (f32[3,2,4,128]{3,2,1,0:T(4,128)S(1)}, f32[3,2,4,128]{3,2,1,0:T(4,128)}, u32[]{:S(2)}) copy-start(f32[3,2,4,128]{3,2,1,0:T(4,128)} %uc.3) | copy-start | bytes 36868
  33.1 2.4 %copy-start.6 = (f32[3,2,4,128]{3,2,1,0:T(4,128)S(1)}, f32[3,2,4,128]{3,2,1,0:T(4,128)}, u32[]{:S(2)}) copy-start(f32[3,2,4,128]{3,2,1,0:T(4,128)} %qc.3) | copy-start | bytes 36868
